TPU v7x, 32 devices: a whole 2x2x4 slice. The times are simulated.
32 devices in a mesh: rep: 4 (over x, core), shard: 8 (over z, y).
Axes of the slice: x: 2, y: 2, z: 4, core: 2. Of those that a mesh axis runs over, the one named last changes fastest.
Arguments:
- outer_delta: float32 [4, 2097152], P('rep', 'shard'), may hold values from -40 to 40
- offsets: int32 [65], replicated, may hold values from 0 to 2097152, as said below
- parameters: float32 [2097152], P('shard'), may hold values from -6 to 6
- momentum: float32 [2097152], P(('shard', 'rep')), may hold values from -1.2 to 1.2
Outputs:
- new_parameters: float32 [2097152], P('shard')
- new_momentum: float32 [2097152], P(('shard', 'rep'))
Inputs may be any that keep to these rules, and one draw needn't show every extreme that they name: `offsets`: strictly increasing multiples of 128, the first 0 and the last 2097152.
All inputs are finite; a program needn't handle non-finite values.
Results may differ from a plain program's by a relative error of at most 0.0003.
Values sent between devices are 32-bit elements; how exact they have to be, the bound alone decides.
A program may use at most 64 MiB of HBM per device.

v0:
```python
import math
import jax
import jax.numpy as jnp
from jax import lax
from jax.sharding import PartitionSpec as P

LR_OUTER = 0.7
MU_OUTER = 0.9
CLIP_RMS = 0.1
EPSILON = 1e-06


def one_hot_rows(first_pos, block_len, offsets):
    tensors = offsets.shape[0] - 1
    positions = first_pos + jnp.arange(block_len, dtype=jnp.int32)
    segment = jnp.sum((positions[:, None] >= offsets[None, 1:tensors]).astype(jnp.int32), axis=1)
    return (segment[:, None] == jnp.arange(tensors, dtype=jnp.int32)[None, :]).astype(jnp.float32)


def tensor_squares(values, first_pos, offsets):
    total_len = values.shape[0]
    block_len = math.gcd(total_len, 8192)
    value_rows = values.reshape(total_len // block_len, block_len)
    block_starts = first_pos + jnp.arange(total_len // block_len, dtype=jnp.int32) * block_len

    def partial_squares(items):
        row_values, row_start = items
        selector = one_hot_rows(row_start, block_len, offsets)
        return jnp.dot(
            row_values * row_values,
            selector,
            precision=lax.Precision.HIGHEST,
            preferred_element_type=jnp.float32,
        )

    return jnp.sum(lax.map(partial_squares, (value_rows, block_starts)), axis=0)


def element_factor(factor, total_len, first_pos, offsets):
    block_len = math.gcd(total_len, 8192)
    block_starts = first_pos + jnp.arange(total_len // block_len, dtype=jnp.int32) * block_len

    def spread_factor(row_start):
        selector = one_hot_rows(row_start, block_len, offsets)
        return jnp.dot(
            selector, factor, precision=lax.Precision.HIGHEST, preferred_element_type=jnp.float32
        )

    return lax.map(spread_factor, block_starts).reshape(total_len)


def clip_factor(squares_sum, offsets):
    lengths = (offsets[1:] - offsets[:-1]).astype(jnp.float32)
    return jnp.minimum(1.0, CLIP_RMS * jnp.sqrt(lengths) * lax.rsqrt(squares_sum + EPSILON))


def on_device(outer_delta, offsets, parameters, momentum):
    replicas = lax.axis_size("rep")
    shard_len = parameters.shape[0]
    own_len = shard_len // replicas
    rep_index = lax.axis_index("rep")
    shard_start = lax.axis_index("shard") * shard_len
    local_delta = outer_delta.reshape(shard_len)
    avg_delta = lax.psum_scatter(local_delta, "rep", scatter_dimension=0, tiled=True) / jnp.float32(
        replicas
    )
    first_pos = shard_start + rep_index * own_len
    squares_sum = lax.psum(tensor_squares(avg_delta, first_pos, offsets), ("shard", "rep"))
    factor = clip_factor(squares_sum, offsets)
    scaled = avg_delta * element_factor(factor, own_len, first_pos, offsets)
    owned_params = lax.dynamic_slice_in_dim(parameters, rep_index * own_len, own_len)
    new_momentum = MU_OUTER * momentum + scaled
    new_owned = owned_params - LR_OUTER * (scaled + MU_OUTER * new_momentum)
    new_parameters = lax.all_gather(new_owned, "rep", axis=0, tiled=True)
    return (new_parameters, new_momentum)


def solution(mesh):
    return jax.shard_map(
        on_device,
        mesh=mesh,
        in_specs=(P("rep", "shard"), P(), P("shard"), P(("shard", "rep"))),
        out_specs=(P("shard"), P(("shard", "rep"))),
        check_vma=False,
    )
```

profile of v0, /device:TPU:0, one launch (start us, length us, event | category | flops | bytes accessed | tf_op | source)
XLA Modules:
  0.0 162.3 jit_solution(8617485549905927681)
XLA Ops:
  7.2 0.7 all-reduce.3.cloned.1.call-update
  8.0 0.7 dynamic-slice
  9.4 40.0 %all-reduce.3.cloned.1.call-done = f32[262144]{0:T(1024)} async-done(((f32[262144]{0:T(1024)}), f32[262144]{0:T(1024)}) %all-reduce.3.cloned.1.call-update) | async-done | bytes 1048592
  49.4 1.0 dynamic-slice_multiply_fusion
  50.4 23.2 %while.20 = (s32[]{:T(128)}, f32[8,64]{1,0:T(8,128)S(1)}, f32[8,8192]{1,0:T(8,128)S(1)}, s32[8]{0:T(128)S(1)}, s32[65]{0:T(128)S(1)}, /*index=5*/s32[]{:T(128)}, s32[]{:T(128)}) while((s32[]{:T(128)}, f32[8,64]{1,0:T(8,128)S(1)}, f32[8,8192]{1,0:T(8,128)S(1)}, s32[8]{0:T(128)S(1)}, s32[65]{0:T(128)S(1)}, /*index=5*/s32[]{:T(128)}, ...), condition=%wide.region_3.4_spmd, body=%wide.region_1.3_spmd.sunk | while | flops 8372226 | bytes 165465 | solution.py:36
  50.5 0.7 dynamic_slice.24
  51.1 0.7 iota_add_fusion.4
  52.2 1.1 fusion.10
  53.4 0.7 dynamic_slice.24
  54.0 0.7 iota_add_fusion.4
  55.1 1.1 fusion.10
  56.3 0.7 dynamic_slice.24
  56.9 0.7 iota_add_fusion.4
  58.0 1.1 fusion.10
  59.2 0.7 dynamic_slice.24
  59.8 0.7 iota_add_fusion.4
  60.9 1.1 fusion.10
  62.1 0.7 dynamic_slice.24
  62.7 0.7 iota_add_fusion.4
  63.8 1.1 fusion.10
  65.0 0.7 dynamic_slice.24
  65.6 0.7 iota_add_fusion.4
  66.8 1.1 fusion.10
  67.9 0.7 dynamic_slice.24
  68.5 0.7 iota_add_fusion.4
  69.7 1.1 fusion.10
  70.8 0.7 dynamic_slice.24
  71.4 0.7 iota_add_fusion.4
  72.6 1.1 fusion.10
  73.7 39.8 %psum.7 = f32[64]{0:T(128)S(1)} all-reduce(f32[64]{0:T(128)S(1)} %reduce_sum.27), channel_id=1, replica_groups=mesh['rep'=4,'shard'=8] {'shard','rep'}, use_global_device_ids=true, to_apply=%region_5.6 | all-reduce | flops 64 | bytes 512 | tf_op jit(solution)/shard_map/psum | solution.py:68
  113.6 20.5 %while.21 = (s32[]{:T(128)}, f32[8,8192]{1,0:T(8,128)S(1)}, s32[8]{0:T(128)S(1)}, s32[65]{0:T(128)S(1)}, f32[64]{0:T(128)S(1)}, /*index=5*/s32[]{:T(128)}, s32[]{:T(128)}) while((s32[]{:T(128)}, f32[8,8192]{1,0:T(8,128)S(1)}, s32[8]{0:T(128)S(1)}, s32[65]{0:T(128)S(1)}, f32[64]{0:T(128)S(1)}, /*index=5*/s32[]{:T(128)}, s32[]{:T(128)}) %tuple.50), condition=%wide.region_8.9_spmd, body=%wide.region_6.8_spmd.sunk | while | flops 8364034 | bytes 230485 | solution.py:49
  114.2 0.6 iota_add_fusion.5
  115.2 0.7 fusion.12
  116.7 0.6 iota_add_fusion.5
  117.8 0.7 fusion.12
  119.3 0.6 iota_add_fusion.5
  120.4 0.7 fusion.12
  122.9 0.7 fusion.12
  124.4 0.6 iota_add_fusion.5
  125.5 0.7 fusion.12
  128.1 0.7 fusion.12
  129.6 0.6 iota_add_fusion.5
  130.6 0.7 fusion.12
  132.1 0.6 iota_add_fusion.5
  133.2 0.7 fusion.12
  134.2 1.9 %multiply_subtract_fusion = (f32[65536]{0:T(1024)}, f32[65536]{0:T(1024)}) fusion(f32[262144]{0:T(1024)} %param.10, s32[]{:T(128)S(6)} %select_n.3, f32[65536]{0:T(1024)S(1)} %copy-done, f32[65536]{0:T(1024)S(1)} %bitcast.24, f32[262144]{0:T(1024)} %all-reduce.3.cloned.1.call-done, u32[]{:T(128)S(6)} %multiply.2), kind=kLoop, calls=%fused_computation.15 | loop fusion | flops 524288 | bytes 1572872 | tf_op jit(solution)/shard_map/sub | solution.py:73
  136.1 17.0 %all-gather.2.cloned.1.call-done = f32[262144]{0:T(1024)} async-done(((f32[65536]{0:T(1024)}), f32[262144]{0:T(1024)}) %all-gather.2.cloned.1.call-update) | async-done | bytes 1048592 | tf_op jit(solution)/shard_map/all_gather | solution.py:74
  153.2 2.3 %copy.24 = f32[262144]{0:T(1024)} copy(f32[262144]{0:T(1024)} %all-gather.2.cloned.1.call-done) | data formatting | bytes 2097152
  (74 shorter events, 14.2 us)
Async XLA Ops:
  7.2 0.8 copy-start.2
  7.2 42.2 %all-reduce.3.cloned.1.call-start = ((), (), s32[]{:S(2)}) async-start(), calls=%async_computation.1 | async-start | bytes 2097152
  7.2 43.2 %copy-start.1 = (s32[65]{0:T(128)S(1)}, s32[65]{0:T(128)}, u32[]{:S(2)}) copy-start(s32[65]{0:T(128)} %param.9) | copy-start | bytes 784
  7.9 145.3 %all-gather.2.cloned.1.call-start = ((), (), s32[]{:S(2)}) async-start(), calls=%async_computation | async-start | bytes 1310720 | tf_op jit(solution)/shard_map/all_gather | solution.py:74
  113.6 20.6 %copy-start = (f32[65536]{0:T(1024)S(1)}, f32[65536]{0:T(1024)}, u32[]{:S(2)}) copy-start(f32[65536]{0:T(1024)} %param.11) | copy-start | bytes 786436
Sparse Core Ops, SparseCore 0:
  10.3 39.0 all-reduce.2
  136.3 16.8 all-gather.1
where the time goes:
time: 163 us; the launch traced here: 162 us
  waiting for transfers between devices  57.7 us (35%)
  blocking collectives  39.8 us (24%)
  other arithmetic  19.1 us (12%)
  local copies, waits for them, and re-layouts  15.6 us (10%)
  between operations  14.9 us (9%)
  matrix products  14.5 us (9%)
    unnamed x3, waiting for transfers between devices  40.7 us
    psum x1, blocking collectives, on_device(): lax.psum(tensor_squares(avg_delta, first_pos, offsets), ('shard', 'rep'))  39.8 us
    all_gather x1, waiting for transfers between devices, on_device(): new_parameters = lax.all_gather(new_owned, 'rep', axis=0, tiled=True)  17 us
    add x16, other arithmetic, one_hot_rows(): positions = first_pos + jnp.arange(block_len, dtype=jnp.int32)  10.7 us
    dynamic_slice x16, local copies, waits for them, and re-layouts, tensor_squares(): return jnp.sum(lax.map(partial_squares, (value_rows, block_starts)), axis=0)  10 us
    dot_general x8, matrix products, partial_squares(): jnp.dot(row_values * row_values, selector, precision=lax.Precision.HIGHES...  8.58 us
    dot_general x8, matrix products, spread_factor(): jnp.dot(selector, factor, precision=lax.Precision.HIGHEST, preferred_elem...  5.97 us
    reduce_sum x16, other arithmetic, one_hot_rows(): jnp.sum((positions[:, None] >= offsets[None, 1:tensors]).astype(jnp.int32...  5.37 us
  transfers between devices with their start and end apart: 2, of which 2 were waited for; matrix products, arithmetic and copies ran while one was open for 0% of the time, Pallas kernels for 0%

commit v1 on v0

--- a/solution.py
+++ b/solution.py
@@ -71,7 +71,14 @@
     owned_params = lax.dynamic_slice_in_dim(parameters, rep_index * own_len, own_len)
     new_momentum = MU_OUTER * momentum + scaled
     new_owned = owned_params - LR_OUTER * (scaled + MU_OUTER * new_momentum)
-    new_parameters = lax.all_gather(new_owned, "rep", axis=0, tiled=True)
+    size = lax.axis_size("rep")
+    hops = [(i, (i + 1) % size) for i in range(size)]
+    terms = [new_owned]
+    for far in range(1, size):
+        terms = [lax.ppermute(terms[0], "rep", hops), *terms]
+    whole = jnp.concatenate(terms, axis=0)
+    shift = (lax.axis_index("rep") + 1) * terms[-1].shape[0]
+    new_parameters = jnp.roll(whole, shift, axis=0)
     return (new_parameters, new_momentum)
 
 

time: 163 us -> 162 us (level)
    ppermute x0 -> x3, waiting for transfers between devices: none -> 17.4 us  [on_device(): terms = [lax.ppermute(terms[0], 'rep', hops), *terms]]
    all_gather x1 -> x0, waiting for transfers between devices: 17 us -> none  [on_device(): new_parameters = lax.all_gather(new_owned, 'rep', axis=0, tiled=True)]
    unnamed x3 -> x2, waiting for transfers between devices: 40.7 us -> 40.1 us
  transfers between devices with their start and end apart: 2 -> 4, of which waited for: 2 -> 4; matrix products, arithmetic and copies ran while one was open for 0% -> 1% of each run, Pallas kernels for 0% -> 0%
where the time goes in v1:
time: 162 us; the launch traced here: 161 us
  waiting for transfers between devices  57.5 us (35%)
  blocking collectives  39.8 us (25%)
  other arithmetic  19 us (12%)
  local copies, waits for them, and re-layouts  15.2 us (9%)
  between operations  14.9 us (9%)
  matrix products  14.5 us (9%)
    unnamed x2, waiting for transfers between devices  40.1 us
    psum x1, blocking collectives, on_device(): lax.psum(tensor_squares(avg_delta, first_pos, offsets), ('shard', 'rep'))  39.8 us
    ppermute x3, waiting for transfers between devices, on_device(): terms = [lax.ppermute(terms[0], 'rep', hops), *terms]  17.4 us
    add x16, other arithmetic, one_hot_rows(): positions = first_pos + jnp.arange(block_len, dtype=jnp.int32)  10.7 us
    dynamic_slice x16, local copies, waits for them, and re-layouts, tensor_squares(): return jnp.sum(lax.map(partial_squares, (value_rows, block_starts)), axis=0)  10 us
    dot_general x8, matrix products, partial_squares(): jnp.dot(row_values * row_values, selector, precision=lax.Precision.HIGHES...  8.58 us
    dot_general x8, matrix products, spread_factor(): jnp.dot(selector, factor, precision=lax.Precision.HIGHEST, preferred_elem...  5.97 us
    reduce_sum x16, other arithmetic, one_hot_rows(): jnp.sum((positions[:, None] >= offsets[None, 1:tensors]).astype(jnp.int32...  5.34 us
  transfers between devices with their start and end apart: 4, of which 4 were waited for; matrix products, arithmetic and copies ran while one was open for 1% of the time, Pallas kernels for 0%

profile of v1, /device:TPU:0, one launch (start us, length us, event | category | flops | bytes accessed | tf_op | source)
XLA Modules:
  0.0 161.5 jit_solution(1326695244506626226)
XLA Ops:
  7.2 0.7 all-reduce.3.cloned.1.call-update
  8.0 1.3 dynamic-slice
  10.0 39.4 %all-reduce.3.cloned.1.call-done = f32[262144]{0:T(1024)} async-done(((f32[262144]{0:T(1024)}), f32[262144]{0:T(1024)}) %all-reduce.3.cloned.1.call-update) | async-done | bytes 1048592
  49.4 1.0 dynamic-slice_multiply_fusion
  50.4 23.2 %while.20 = (s32[]{:T(128)}, f32[8,64]{1,0:T(8,128)S(1)}, f32[8,8192]{1,0:T(8,128)S(1)}, s32[8]{0:T(128)S(1)}, s32[65]{0:T(128)S(1)}, /*index=5*/s32[]{:T(128)}, s32[]{:T(128)}) while((s32[]{:T(128)}, f32[8,64]{1,0:T(8,128)S(1)}, f32[8,8192]{1,0:T(8,128)S(1)}, s32[8]{0:T(128)S(1)}, s32[65]{0:T(128)S(1)}, /*index=5*/s32[]{:T(128)}, ...), condition=%wide.region_3.4_spmd, body=%wide.region_1.3_spmd.sunk | while | flops 8372226 | bytes 165473 | solution.py:36
  50.5 0.7 dynamic_slice.29
  51.2 0.7 iota_add_fusion.4
  52.2 1.1 fusion.10
  53.4 0.7 dynamic_slice.29
  54.1 0.7 iota_add_fusion.4
  55.1 1.1 fusion.10
  56.3 0.7 dynamic_slice.29
  57.0 0.7 iota_add_fusion.4
  58.0 1.1 fusion.10
  59.2 0.7 dynamic_slice.29
  59.9 0.7 iota_add_fusion.4
  60.9 1.1 fusion.10
  62.1 0.7 dynamic_slice.29
  62.8 0.7 iota_add_fusion.4
  63.8 1.1 fusion.10
  65.0 0.7 dynamic_slice.29
  65.7 0.7 iota_add_fusion.4
  66.7 1.1 fusion.10
  67.9 0.7 dynamic_slice.29
  68.6 0.7 iota_add_fusion.4
  69.6 1.1 fusion.10
  70.8 0.7 dynamic_slice.29
  71.5 0.7 iota_add_fusion.4
  72.5 1.1 fusion.10
  73.7 39.8 %psum.7 = f32[64]{0:T(128)S(1)} all-reduce(f32[64]{0:T(128)S(1)} %reduce_sum.27), channel_id=1, replica_groups=mesh['rep'=4,'shard'=8] {'shard','rep'}, use_global_device_ids=true, to_apply=%region_5.6 | all-reduce | flops 64 | bytes 512 | tf_op jit(solution)/shard_map/psum | solution.py:68
  113.5 20.5 %while.21 = (s32[]{:T(128)}, f32[8,8192]{1,0:T(8,128)S(1)}, s32[8]{0:T(128)S(1)}, s32[65]{0:T(128)S(1)}, f32[64]{0:T(128)S(1)}, /*index=5*/s32[]{:T(128)}, s32[]{:T(128)}) while((s32[]{:T(128)}, f32[8,8192]{1,0:T(8,128)S(1)}, s32[8]{0:T(128)S(1)}, s32[65]{0:T(128)S(1)}, f32[64]{0:T(128)S(1)}, /*index=5*/s32[]{:T(128)}, s32[]{:T(128)}) %tuple.46), condition=%wide.region_8.9_spmd, body=%wide.region_6.8_spmd.sunk | while | flops 8364034 | bytes 230493 | solution.py:49
  114.2 0.6 iota_add_fusion.5
  115.2 0.7 fusion.12
  117.8 0.7 fusion.12
  119.3 0.6 iota_add_fusion.5
  120.3 0.7 fusion.12
  121.9 0.6 iota_add_fusion.5
  122.9 0.7 fusion.12
  124.5 0.6 iota_add_fusion.5
  125.5 0.7 fusion.12
  128.0 0.7 fusion.12
  130.6 0.7 fusion.12
  133.2 0.7 fusion.12
  134.1 1.8 %multiply_subtract_fusion = (f32[65536]{0:T(1024)S(1)}, f32[65536]{0:T(1024)}) fusion(f32[262144]{0:T(1024)} %param.10, s32[]{:T(128)S(6)} %select_n.16, f32[65536]{0:T(1024)S(1)} %copy-done, f32[65536]{0:T(1024)S(1)} %bitcast.24, f32[262144]{0:T(1024)} %all-reduce.3.cloned.1.call-done, u32[]{:T(128)S(6)} %multiply.2), kind=kLoop, calls=%fused_computation.15 | loop fusion | flops 524288 | bytes 1572872 | tf_op jit(solution)/shard_map/sub | solution.py:73
  136.0 5.8 %collective-permute-done = f32[65536]{0:T(1024)S(1)} collective-permute-done((f32[65536]{0:T(1024)S(1)}, f32[65536]{0:T(1024)S(1)}, u32[]{:S(2)}, u32[]{:S(2)}) %collective-permute-start) | collective-permute-done | bytes 262176 | tf_op jit(solution)/shard_map/ppermute | solution.py:78
  141.8 5.8 %collective-permute-done.1 = f32[65536]{0:T(1024)S(1)} collective-permute-done((f32[65536]{0:T(1024)S(1)}, f32[65536]{0:T(1024)S(1)}, u32[]{:S(2)}, u32[]{:S(2)}) %collective-permute-start.1) | collective-permute-done | bytes 262176 | tf_op jit(solution)/shard_map/ppermute | solution.py:78
  147.6 5.8 %collective-permute-done.2 = f32[65536]{0:T(1024)S(1)} collective-permute-done((f32[65536]{0:T(1024)S(1)}, f32[65536]{0:T(1024)S(1)}, u32[]{:S(2)}, u32[]{:S(2)}) %collective-permute-start.2) | collective-permute-done | bytes 262176 | tf_op jit(solution)/shard_map/ppermute | solution.py:78
  153.6 1.0 dynamic_slice.19
  (83 shorter events, 15.6 us)
Async XLA Ops:
  7.2 43.3 %copy-start.1 = (s32[65]{0:T(128)S(1)}, s32[65]{0:T(128)}, u32[]{:S(2)}) copy-start(s32[65]{0:T(128)} %param.9) | copy-start | bytes 784
  7.2 42.2 %all-reduce.3.cloned.1.call-start = ((), (), s32[]{:S(2)}) async-start(), calls=%async_computation | async-start | bytes 2097152
  73.7 60.5 %copy-start = (f32[65536]{0:T(1024)S(1)}, f32[65536]{0:T(1024)}, u32[]{:S(2)}) copy-start(f32[65536]{0:T(1024)} %param.11) | copy-start | bytes 786436
  136.0 5.8 %collective-permute-start = (f32[65536]{0:T(1024)S(1)}, f32[65536]{0:T(1024)S(1)}, u32[]{:S(2)}, u32[]{:S(2)}) collective-permute-start(f32[65536]{0:T(1024)S(1)} %get-tuple-element.78), channel_id=1, source_target_pairs={{0,8},{8,16},{16,24},{24,0},{1,9},{9,17},{17,25},{25,1},{2,10},{10... | collective-permute-start | bytes 786440 | tf_op jit(solution)/shard_map/ppermute | solution.py:78
  141.8 5.8 %collective-permute-start.1 = (f32[65536]{0:T(1024)S(1)}, f32[65536]{0:T(1024)S(1)}, u32[]{:S(2)}, u32[]{:S(2)}) collective-permute-start(f32[65536]{0:T(1024)S(1)} %collective-permute-done), channel_id=1, source_target_pairs={{0,8},{8,16},{16,24},{24,0},{1,9},{9,17},{17,25},{25,1},{2,10},{10... | collective-permute-start | bytes 786440 | tf_op jit(solution)/shard_map/ppermute | solution.py:78
  147.6 5.8 %collective-permute-start.2 = (f32[65536]{0:T(1024)S(1)}, f32[65536]{0:T(1024)S(1)}, u32[]{:S(2)}, u32[]{:S(2)}) collective-permute-start(f32[65536]{0:T(1024)S(1)} %collective-permute-done.1), channel_id=1, source_target_pairs={{0,8},{8,16},{16,24},{24,0},{1,9},{9,17},{17,25},{25,1},{2,10},{10... | collective-permute-start | bytes 786440 | tf_op jit(solution)/shard_map/ppermute | solution.py:78
Sparse Core Ops, SparseCore 0:
  10.3 39.0 all-reduce.2
